TPU v7x, 512 devices: a whole 4x8x8 slice. The times are simulated.
512 devices in a mesh: fluid: 64 (over z, x, core), solid: 8 (over y).
Axes of the slice: x: 4, y: 8, z: 8, core: 2. Of those that a mesh axis runs over, the one named last changes fastest.
Arguments:
- fluid_load: float32 [32768, 3, 128], P(('fluid', 'solid')), may hold values from -6 to 6
- stiffness: float32 [32768, 3, 128], P(('fluid', 'solid')), may hold values from 0.2 to 2
- mapping: bfloat16 [32768, 128, 128], P(('fluid', 'solid')), may hold values from -0.5 to 0.5
- live_count: int32 [512], P(('fluid', 'solid')), may hold values from 40 to 64, as said below
- dest_device: int32 [32768, 1], P(('fluid', 'solid')), may hold values from 0 to 63; in each aligned block of 64 rows (0 to 63, 64 to 127, ...) at most 2 rows name the same one
- local_block: int32 [32768], P(('fluid', 'solid')), may hold values from 0 to 3
- compliance: float32 [8, 256, 3, 128], P('solid', 'fluid'), may hold values from 0.05 to 0.5
- start_disp: float32 [8, 256, 3, 128], P('solid', 'fluid'), may hold values from -40 to 40
- residual_history: float32 [50, 8, 256, 3, 128], P(None, 'solid', 'fluid'), may hold values from -40 to 40
- update_history: float32 [50, 8, 256, 3, 128], P(None, 'solid', 'fluid'), may hold values from -2.4 to 2.4
Outputs:
- displacement: float32 [8, 256, 3, 128], P('solid', 'fluid')
- fluid_displacement: float32 [32768, 3, 128], P(('fluid', 'solid'))
Inputs may be any that keep to these rules, and one draw needn't show every extreme that they name: `live_count`: each device's live blocks are its first ones; some device has exactly 64. `dest_device`: among the 64 rows of one device no fluid index appears more than 2 times.
All inputs are finite; a program needn't handle non-finite values.
Results may differ from a plain program's by a relative error of at most 0.0094.
Values may be sent and summed in bfloat16 or wider, within the bound.
No kernel may reach another device: no remote copies, remote signals or barrier semaphores. Data moves between devices by JAX's collectives and lax.ppermute only.
A program may use at most 64 MiB of HBM per device.

v0:
```python
import jax
import jax.numpy as jnp
from jax import lax
from jax.sharding import Mesh
from jax.sharding import PartitionSpec as P

ITERS = 2
FLUID_SOLID = ("fluid_0", "fluid_1", "fluid_2", "solid")
FLUID = ("fluid_0", "fluid_1", "fluid_2")
ridge_share = 0.01


def over_axes(x, axes):
    for axis in axes:
        x = lax.psum(x, axis)
    return x


def sent_to_all(x, axis):
    copies = jnp.broadcast_to(x, (lax.axis_size(axis), *x.shape))
    return lax.all_to_all(copies, axis, split_axis=0, concat_axis=0, tiled=True)


def in_order(parts, dim):
    dims = list(parts.shape[1:])
    dims[dim] *= parts.shape[0]
    return jnp.moveaxis(parts, 0, dim).reshape(dims)


def gathered_copies(x, axis, dim):
    parts = sent_to_all(x, axis)
    return in_order(parts, dim)


def in_blocks(x, dim, count):
    before, after = (x.shape[:dim], x.shape[dim + 1 :])
    return jnp.moveaxis(x.reshape(*before, count, -1, *after), dim, 0)


def sum_at_owner(x, axis, dim):
    count = lax.axis_size(axis)
    parts = lax.all_to_all(in_blocks(x, dim, count), axis, 0, 0, tiled=True)
    return jnp.sum(parts.astype(jnp.float32), axis=0)


def solve_small(gram_matrix, right_side):
    order = gram_matrix.shape[0]
    ridge = ridge_share * jnp.trace(gram_matrix) / order
    factor = jnp.linalg.cholesky(gram_matrix + ridge * jnp.eye(order, dtype=gram_matrix.dtype))
    halfway = lax.linalg.triangular_solve(factor, right_side[:, None], left_side=True, lower=True)
    solved = lax.linalg.triangular_solve(
        factor, halfway, left_side=True, lower=True, transpose_a=True
    )
    return -solved[:, 0]


def full_sums(basis_flat, resid_flat):
    gram_local = jnp.dot(basis_flat, basis_flat.T, precision=lax.Precision.HIGHEST)
    right_local = jnp.dot(basis_flat, resid_flat, precision=lax.Precision.HIGHEST)
    return (over_axes(gram_local, FLUID_SOLID), over_axes(right_local, FLUID_SOLID))


def body(
    fluid_load,
    stiffness,
    mapping,
    live_count,
    dest_device,
    local_block,
    compliance,
    start_disp,
    residual_history,
    update_history,
):
    blocks = mapping.shape[0]
    sub_blocks = compliance.shape[1]
    alive = (jnp.arange(blocks) < live_count[0]).astype(jnp.float32)[:, None, None]
    target = dest_device[:, 0] * sub_blocks + local_block

    def to_fluid(struct_disp):
        packed = struct_disp[0].astype(jnp.bfloat16)
        pieces = gathered_copies(packed, FLUID, 0)
        onehot = (target[:, None] == jnp.arange(pieces.shape[0])[None, :]).astype(jnp.bfloat16)
        picked = jnp.einsum("bk,kcj->bcj", onehot, pieces, preferred_element_type=jnp.float32)
        fluid_disp = jnp.einsum(
            "bjn,bcj->bcn", mapping, picked.astype(jnp.bfloat16), preferred_element_type=jnp.float32
        )
        return fluid_disp * alive

    struct_disp = start_disp
    basis_cols = residual_history
    updates = update_history
    last_resid = struct_disp
    last_image = struct_disp
    gram_matrix = None
    for iteration in range(ITERS):
        fluid_disp = to_fluid(struct_disp)
        fluid_force = (alive * (fluid_load - stiffness * fluid_disp)).astype(jnp.bfloat16)
        contrib = jnp.einsum(
            "bjn,bcn->bcj", mapping, fluid_force, preferred_element_type=jnp.float32
        )
        force_onehot = (
            jnp.arange(sub_blocks * lax.axis_size(FLUID))[:, None] == target[None, :]
        ).astype(jnp.float32)
        summed = sum_at_owner(
            jnp.einsum(
                "rb,bcj->rcj", force_onehot, contrib, precision=lax.Precision.HIGHEST
            ).astype(jnp.bfloat16),
            FLUID,
            0,
        )
        struct_image = compliance * summed[None]
        residual = struct_image - struct_disp
        newest = residual - last_resid
        if iteration > 0:
            basis_cols = jnp.concatenate([basis_cols[1:], newest[None]], 0)
            updates = jnp.concatenate([updates[1:], (struct_image - last_image)[None]], 0)
        basis_flat = basis_cols.reshape(basis_cols.shape[0], -1)
        resid_flat = residual.reshape(-1)
        if iteration == 0:
            gram_matrix, right_side = full_sums(basis_flat, resid_flat)
        else:
            row_local = jnp.dot(basis_flat, newest.reshape(-1), precision=lax.Precision.HIGHEST)
            right_local = jnp.dot(basis_flat, resid_flat, precision=lax.Precision.HIGHEST)
            new_row, right_side = (
                over_axes(row_local, FLUID_SOLID),
                over_axes(right_local, FLUID_SOLID),
            )
            upper_part = jnp.concatenate([gram_matrix[1:, 1:], new_row[:-1, None]], 1)
            gram_matrix = jnp.concatenate([upper_part, new_row[None, :]], 0)
        coefficients = solve_small(gram_matrix, right_side)
        struct_disp = struct_image + jnp.tensordot(
            coefficients, updates, axes=1, precision=lax.Precision.HIGHEST
        )
        last_resid = residual
        last_image = struct_image
    final_disp = to_fluid(struct_disp)
    return (struct_disp, final_disp)


def solution(mesh):
    split = Mesh(
        mesh.devices.reshape(8, 4, 2, mesh.shape["solid"]),
        ("fluid_0", "fluid_1", "fluid_2", "solid"),
    )
    in_specs = (
        P(FLUID_SOLID, None, None),
        P(FLUID_SOLID, None, None),
        P(FLUID_SOLID, None, None),
        P(FLUID_SOLID),
        P(FLUID_SOLID, None),
        P(FLUID_SOLID),
        P("solid", FLUID, None, None),
        P("solid", FLUID, None, None),
        P(None, "solid", FLUID, None, None),
        P(None, "solid", FLUID, None, None),
    )
    out_specs = (P("solid", FLUID, None, None), P(FLUID_SOLID, None, None))
    return jax.shard_map(body, mesh=split, in_specs=in_specs, out_specs=out_specs, check_vma=False)
```

profile of v0, /device:TPU:1, one launch (start us, length us, event | category | flops | bytes accessed | tf_op | source)
XLA Modules:
  0.0 251.1 jit_solution(15389651478953611320)
XLA Ops:
  0.6 0.8 convert_bitcast_fusion.2
  1.5 0.7 broadcast_in_dim.50
  2.2 14.8 %all-to-all-start = ((bf16[64,4,3,128]{3,1,2,0:T(4,128)(2,1)}), bf16[64,4,3,128]{3,1,2,0:T(4,128)(2,1)S(1)}, u32[]{:S(2)}, u32[]{:S(2)}) async-start(bf16[64,4,3,128]{3,1,2,0:T(4,128)(2,1)} %broadcast_in_dim.50), calls=%async_computation | async-start | bytes 393216 | tf_op jit(solution)/shard_map/all_to_all | solution.py:21
  17.7 0.7 bitcast_add_fusion.2
  18.4 10.7 %all-to-all-done = bf16[64,4,3,128]{3,1,2,0:T(4,128)(2,1)S(1)} async-done(((bf16[64,4,3,128]{3,1,2,0:T(4,128)(2,1)}), bf16[64,4,3,128]{3,1,2,0:T(4,128)(2,1)S(1)}, u32[]{:S(2)}, u32[]{:S(2)}) %all-to-all-start) | async-done | bytes 196640 | tf_op jit(solution)/shard_map/all_to_all | solution.py:21
  29.0 0.1 copy.39
  29.1 0.2 convolution_convert_fusion.4
  29.4 2.7 %fusion.9 = f32[64,3,128]{2,1,0:T(4,128)S(1)} fusion(bf16[64,128,128]{2,1,0:T(8,128)(2,1)S(1)} %copy-done, f32[64,3,128]{2,0,1:T(8,128)} %param.15, f32[64,3,128]{2,0,1:T(8,128)} %param.16, bf16[64,3,128]{2,0,1:T(8,128)(2,1)S(1)} %convolution_convert_fusion.4, f32[64]{0:T(128)S(1)} %compare_convert_fusion), kind=kOutput, calls=%fused_computation.17 | convolution fusion | flops 12705792 | bytes 2441472 | tf_op jit(solution)/shard_map/bjn,bcn->bcj/dot_general | solution.py:99
  32.1 0.5 convolution_convert_fusion.1
  32.5 0.7 copy.44
  33.3 4.5 %all-to-all-start.1 = ((bf16[64,4,3,128]{3,1,2,0:T(4,128)(2,1)}), bf16[64,4,3,128]{3,1,2,0:T(4,128)(2,1)S(1)}, u32[]{:S(2)}, u32[]{:S(2)}) async-start(bf16[64,4,3,128]{3,1,2,0:T(4,128)(2,1)} %copy.44), calls=%async_computation.1 | async-start | bytes 393216 | tf_op jit(solution)/shard_map/all_to_all | solution.py:42
  37.8 0.4 convolution_bitcast_fusion
  38.2 11.7 %all-to-all-done.1 = bf16[64,4,3,128]{3,1,2,0:T(4,128)(2,1)S(1)} async-done(((bf16[64,4,3,128]{3,1,2,0:T(4,128)(2,1)}), bf16[64,4,3,128]{3,1,2,0:T(4,128)(2,1)S(1)}, u32[]{:S(2)}, u32[]{:S(2)}) %all-to-all-start.1) | async-done | bytes 196640 | tf_op jit(solution)/shard_map/all_to_all | solution.py:42
  49.9 0.1 convert_reduce_fusion.1
  50.1 0.4 convolution_bitcast_fusion.3
  50.4 21.0 %all-reduce.3 = (f32[50]{0:T(128)S(1)}, f32[50,50]{0,1:T(8,128)S(1)}) all-reduce(f32[50]{0:T(128)S(1)} %convolution_bitcast_fusion.3, f32[50,50]{0,1:T(8,128)S(1)} %convolution_bitcast_fusion), channel_id=1, replica_groups=mesh['fluid_0'=8,'fluid_1'=4,'fluid_2'=2,'solid'=8] {'fluid_0'}, use_global_device_ids=true, to_apply=%region_8.10 | all-reduce | flops 2550 | bytes 20400 | tf_op jit(solution)/shard_map/psum | solution.py:15
  71.4 11.7 %all-reduce.5 = (f32[50]{0:T(128)S(1)}, f32[50,50]{0,1:T(8,128)S(1)}) all-reduce(f32[50]{0:T(128)S(1)} %get-tuple-element.17, f32[50,50]{0,1:T(8,128)S(1)} %get-tuple-element.18), channel_id=1, replica_groups=mesh['fluid_0'=8,'fluid_1'=4,'fluid_2'=2,'solid'=8] {'fluid_1'}, use_global_device_ids=true, to_apply=%region_9.0 | all-reduce | flops 2550 | bytes 20400 | tf_op jit(solution)/shard_map/psum | solution.py:15
  83.1 14.6 %all-reduce.7 = (f32[50]{0:T(128)S(1)}, f32[50,50]{0,1:T(8,128)S(1)}) all-reduce(f32[50]{0:T(128)S(1)} %get-tuple-element.21, f32[50,50]{0,1:T(8,128)S(1)} %get-tuple-element.22), channel_id=1, replica_groups=mesh['fluid_0'=8,'fluid_1'=4,'fluid_2'=2,'solid'=8] {'fluid_2'}, use_global_device_ids=true, to_apply=%region_10.12 | all-reduce | flops 2550 | bytes 20400 | tf_op jit(solution)/shard_map/psum | solution.py:15
  97.7 23.2 %all-reduce.1 = (f32[50,1]{0,1:T(1,128)S(1)}, f32[50,50]{0,1:T(8,128)S(1)}) all-reduce(f32[50,1]{0,1:T(1,128)S(1)} %bitcast.163, f32[50,50]{0,1:T(8,128)S(1)} %get-tuple-element.26), channel_id=1, replica_groups=mesh['fluid_0'=8,'fluid_1'=4,'fluid_2'=2,'solid'=8] {'solid'}, use_global_device_ids=true, to_apply=%region_11.13 | all-reduce | flops 2550 | bytes 20400 | tf_op jit(solution)/shard_map/psum | solution.py:15
  120.9 0.6 select_reduce_fusion.3
  122.1 0.1 copy.48
  122.3 4.6 %cholesky.44 = f32[50,50]{1,0:T(8,128)S(1)} custom-call(f32[50,50]{1,0:T(8,128)S(1)} %fusion.54), custom_call_target="Cholesky" | custom-call | tf_op jit(solution)/shard_map/jit(cholesky)/cholesky | solution.py:49
  126.9 0.6 compare_reduce_fusion.1
  127.5 0.7 fusion.47
  128.2 3.8 %custom-call.11 = f32[1,50,50]{1,2,0:T(8,128)S(1)} custom-call(f32[1,50,50]{2,1,0:T(8,128)S(1)} %fusion.47), custom_call_target="InvertDiagBlocksLowerTriangular" | custom-call | tf_op jit(solution)/shard_map/triangular_solve/custom-call.2 | solution.py:51
  132.0 0.2 convolution_bitcast_fusion.7
  132.1 0.2 fusion.13
  132.3 0.3 fusion.16
  132.7 24.8 %all_to_all.25 = bf16[64,4,3,128]{3,1,2,0:T(4,128)(2,1)S(1)} all-to-all(bf16[64,4,3,128]{3,1,2,0:T(4,128)(2,1)S(1)} %broadcast_in_dim.54), channel_id=1, replica_groups=mesh['fluid_0'=8,'fluid_1'=4,'fluid_2'=2,'solid'=8] {'fluid_0','fluid_1'..., dimensions={0} | all-to-all | bytes 393216 | tf_op jit(solution)/shard_map/all_to_all | solution.py:21
  157.5 0.1 copy.49
  157.6 0.2 convolution_convert_fusion.3
  157.8 1.7 fusion.8
  159.6 0.5 convolution_convert_fusion
  160.0 0.7 copy.54
  160.8 4.5 %all-to-all-start.3 = ((bf16[64,4,3,128]{3,1,2,0:T(4,128)(2,1)}), bf16[64,4,3,128]{3,1,2,0:T(4,128)(2,1)S(1)}, u32[]{:S(2)}, u32[]{:S(2)}) async-start(bf16[64,4,3,128]{3,1,2,0:T(4,128)(2,1)} %copy.54), calls=%async_computation.3 | async-start | bytes 393216 | tf_op jit(solution)/shard_map/all_to_all | solution.py:42
  165.3 0.1 slice.24
  165.4 12.0 %all-to-all-done.3 = bf16[64,4,3,128]{3,1,2,0:T(4,128)(2,1)S(1)} async-done(((bf16[64,4,3,128]{3,1,2,0:T(4,128)(2,1)}), bf16[64,4,3,128]{3,1,2,0:T(4,128)(2,1)S(1)}, u32[]{:S(2)}, u32[]{:S(2)}) %all-to-all-start.3) | async-done | bytes 196640 | tf_op jit(solution)/shard_map/all_to_all | solution.py:42
  177.4 0.1 convert_reduce_fusion
  177.5 0.1 maximum_bitcast_fusion
  177.6 0.4 convolution_bitcast_fusion.1
  178.0 0.4 convolution_bitcast_fusion.2
  178.4 11.9 %all-reduce.2 = (f32[50]{0:T(128)S(1)}, f32[50]{0:T(128)S(1)}) all-reduce(f32[50]{0:T(128)S(1)} %convolution_bitcast_fusion.1, f32[50]{0:T(128)S(1)} %convolution_bitcast_fusion.2), channel_id=1, replica_groups=mesh['fluid_0'=8,'fluid_1'=4,'fluid_2'=2,'solid'=8] {'fluid_0'}, use_global_device_ids=true, to_apply=%region_18.0 | all-reduce | flops 100 | bytes 800 | tf_op jit(solution)/shard_map/psum | solution.py:15
  190.2 6.5 %all-reduce.4 = (f32[50]{0:T(128)S(1)}, f32[50]{0:T(128)S(1)}) all-reduce(f32[50]{0:T(128)S(1)} %get-tuple-element.15, f32[50]{0:T(128)S(1)} %get-tuple-element.16), channel_id=1, replica_groups=mesh['fluid_0'=8,'fluid_1'=4,'fluid_2'=2,'solid'=8] {'fluid_1'}, use_global_device_ids=true, to_apply=%region_19.23 | all-reduce | flops 100 | bytes 800 | tf_op jit(solution)/shard_map/psum | solution.py:15
  196.8 8.5 %all-reduce.6 = (f32[50]{0:T(128)S(1)}, f32[50]{0:T(128)S(1)}) all-reduce(f32[50]{0:T(128)S(1)} %get-tuple-element.19, f32[50]{0:T(128)S(1)} %get-tuple-element.20), channel_id=1, replica_groups=mesh['fluid_0'=8,'fluid_1'=4,'fluid_2'=2,'solid'=8] {'fluid_2'}, use_global_device_ids=true, to_apply=%region_20.24 | all-reduce | flops 100 | bytes 800 | tf_op jit(solution)/shard_map/psum | solution.py:15
  205.3 10.8 %all-reduce = (f32[50,1]{0,1:T(1,128)S(1)}, f32[50]{0:T(128)S(1)}) all-reduce(f32[50,1]{0,1:T(1,128)S(1)} %bitcast.165, f32[50]{0:T(128)S(1)} %get-tuple-element.24), channel_id=1, replica_groups=mesh['fluid_0'=8,'fluid_1'=4,'fluid_2'=2,'solid'=8] {'solid'}, use_global_device_ids=true, to_apply=%region_21.25 | all-reduce | flops 100 | bytes 800 | tf_op jit(solution)/shard_map/psum | solution.py:15
  216.0 0.1 copy.55
  216.1 0.7 select_reduce_fusion.2
  217.5 0.1 select_add_fusion
  217.6 0.1 copy.56
  217.7 0.1 fusion.51
  217.7 4.6 %cholesky.55 = f32[50,50]{1,0:T(8,128)S(1)} custom-call(f32[50,50]{1,0:T(8,128)S(1)} %fusion.51), custom_call_target="Cholesky" | custom-call | tf_op jit(solution)/shard_map/jit(cholesky)/cholesky | solution.py:49
  222.3 0.6 compare_reduce_fusion
  223.0 0.7 fusion.48
  223.6 3.8 %custom-call.13 = f32[1,50,50]{1,2,0:T(8,128)S(1)} custom-call(f32[1,50,50]{2,1,0:T(8,128)S(1)} %fusion.48), custom_call_target="InvertDiagBlocksLowerTriangular" | custom-call | tf_op jit(solution)/shard_map/triangular_solve/custom-call.2 | solution.py:51
  227.5 0.2 convolution_bitcast_fusion.5
  227.6 0.2 fusion.11
  227.8 0.1 maximum_bitcast_fusion.1
  227.9 0.3 fusion.14
  228.2 0.6 convert_bitcast_fusion
  228.8 20.7 %all_to_all.26 = bf16[64,4,3,128]{3,1,2,0:T(4,128)(2,1)S(1)} all-to-all(bf16[64,4,3,128]{3,1,2,0:T(4,128)(2,1)S(1)} %broadcast_in_dim.61), channel_id=1, replica_groups=mesh['fluid_0'=8,'fluid_1'=4,'fluid_2'=2,'solid'=8] {'fluid_0','fluid_1'..., dimensions={0} | all-to-all | bytes 393216 | tf_op jit(solution)/shard_map/all_to_all | solution.py:21
  249.6 0.1 copy.57
  249.6 0.2 convolution_convert_fusion.2
  249.8 0.7 convolution_multiply_fusion
  250.5 0.7 copy.59
  (28 shorter events, 0.3 us)
Async XLA Ops:
  0.6 28.7 %copy-start = (bf16[64,128,128]{2,1,0:T(8,128)(2,1)S(1)}, bf16[64,128,128]{2,1,0:T(8,128)(2,1)}, u32[]{:S(2)}) copy-start(bf16[64,128,128]{2,1,0:T(8,128)(2,1)} %param.17) | copy-start | bytes 6291460
  2.2 26.8 %all-to-all-start = ((bf16[64,4,3,128]{3,1,2,0:T(4,128)(2,1)}), bf16[64,4,3,128]{3,1,2,0:T(4,128)(2,1)S(1)}, u32[]{:S(2)}, u32[]{:S(2)}) async-start(bf16[64,4,3,128]{3,1,2,0:T(4,128)(2,1)} %broadcast_in_dim.50), calls=%async_computation | async-start | bytes 393216 | tf_op jit(solution)/shard_map/all_to_all | solution.py:21
  29.3 8.4 %copy-start.1 = (f32[50,1,4,3,128]{4,2,3,1,0:T(4,128)S(1)}, f32[50,1,4,3,128]{4,2,3,1,0:T(4,128)}, u32[]{:S(2)}) copy-start(f32[50,1,4,3,128]{4,2,3,1,0:T(4,128)} %param.23) | copy-start | bytes 921604
  29.4 20.7 %copy-start.5 = (f32[1,4,3,128]{3,1,2,0:T(4,128)S(1)}, f32[1,4,3,128]{3,1,2,0:T(4,128)}, u32[]{:S(2)}) copy-start(f32[1,4,3,128]{3,1,2,0:T(4,128)} %param.21) | copy-start | bytes 18436
  29.4 20.7 %copy-start.6 = (f32[1,4,3,128]{3,1,2,0:T(4,128)S(1)}, f32[1,4,3,128]{3,1,2,0:T(4,128)}, u32[]{:S(2)}) copy-start(f32[1,4,3,128]{3,1,2,0:T(4,128)} %param.22) | copy-start | bytes 18436
  32.1 100.2 %copy-start.2 = (f32[50,1,4,3,128]{4,2,3,1,0:T(4,128)S(1)}, f32[50,1,4,3,128]{4,2,3,1,0:T(4,128)}, u32[]{:S(2)}) copy-start(f32[50,1,4,3,128]{4,2,3,1,0:T(4,128)} %param.24) | copy-start | bytes 921604
  32.1 125.8 %copy-start.3 = (f32[64,3,128]{2,0,1:T(8,128)S(1)}, f32[64,3,128]{2,0,1:T(8,128)}, u32[]{:S(2)}) copy-start(f32[64,3,128]{2,0,1:T(8,128)} %param.15) | copy-start | bytes 294916
  32.1 125.8 %copy-start.4 = (f32[64,3,128]{2,0,1:T(8,128)S(1)}, f32[64,3,128]{2,0,1:T(8,128)}, u32[]{:S(2)}) copy-start(f32[64,3,128]{2,0,1:T(8,128)} %param.16) | copy-start | bytes 294916
  33.3 16.6 %all-to-all-start.1 = ((bf16[64,4,3,128]{3,1,2,0:T(4,128)(2,1)}), bf16[64,4,3,128]{3,1,2,0:T(4,128)(2,1)S(1)}, u32[]{:S(2)}, u32[]{:S(2)}) async-start(bf16[64,4,3,128]{3,1,2,0:T(4,128)(2,1)} %copy.44), calls=%async_computation.1 | async-start | bytes 393216 | tf_op jit(solution)/shard_map/all_to_all | solution.py:42
  160.8 16.6 %all-to-all-start.3 = ((bf16[64,4,3,128]{3,1,2,0:T(4,128)(2,1)}), bf16[64,4,3,128]{3,1,2,0:T(4,128)(2,1)S(1)}, u32[]{:S(2)}, u32[]{:S(2)}) async-start(bf16[64,4,3,128]{3,1,2,0:T(4,128)(2,1)} %copy.54), calls=%async_computation.3 | async-start | bytes 393216 | tf_op jit(solution)/shard_map/all_to_all | solution.py:42
where the time goes:
time: 252 us; the launch traced here: 251 us
  blocking collectives  154 us (61%)
  waiting for transfers between devices  34.4 us (14%)
  starting transfers between devices  23.8 us (9%)
  other arithmetic  23.5 us (9%)
  matrix products  9.37 us (4%)
  local copies, waits for them, and re-layouts  3.67 us (1%)
  between operations  2.85 us (1%)
    psum x8, blocking collectives, over_axes(): x = lax.psum(x, axis)  108 us
    all_to_all x2, blocking collectives, sent_to_all(): return lax.all_to_all(copies, axis, split_axis=0, concat_axis=0, tiled=True)  45.6 us
    all_to_all x2, waiting for transfers between devices, sum_at_owner(): parts = lax.all_to_all(in_blocks(x, dim, count), axis, 0, 0, tiled=True)  23.7 us
    all_to_all x1, starting transfers between devices, sent_to_all(): return lax.all_to_all(copies, axis, split_axis=0, concat_axis=0, tiled=True)  14.8 us
    all_to_all x1, waiting for transfers between devices, sent_to_all(): return lax.all_to_all(copies, axis, split_axis=0, concat_axis=0, tiled=True)  10.7 us
    another operation x6, other arithmetic, solve_small(): jnp.linalg.cholesky(gram_matrix + ridge * jnp.eye(order, dtype=gram_matri...  10.5 us
    another operation x4, other arithmetic, solve_small(): lax.linalg.triangular_solve(factor, halfway, left_side=True, lower=True,...  8.96 us
    all_to_all x2, starting transfers between devices, sum_at_owner(): parts = lax.all_to_all(in_blocks(x, dim, count), axis, 0, 0, tiled=True)  8.93 us
  transfers between devices with their start and end apart: 3, of which 3 were waited for; matrix products, arithmetic and copies ran while one was open for 0% of the time, Pallas kernels for 0%

commit v1 on v0

--- a/solution.py
+++ b/solution.py
@@ -12,7 +12,7 @@
 
 def over_axes(x, axes):
     for axis in axes:
-        x = lax.psum(x, axis)
+        x = jnp.sum(lax.all_gather(x, axis), axis=0)
     return x
 
 

time: 252 us -> 281 us (1.12)
  blocking collectives: 154 us -> 183 us
  waiting for transfers between devices: 34.4 us -> 12.1 us
  starting transfers between devices: 23.8 us -> 34.2 us
  local copies, waits for them, and re-layouts: 3.67 us -> 12.8 us
    psum x8 -> x0, blocking collectives: 108 us -> none  [over_axes(): x = lax.psum(x, axis)]
    unnamed x0 -> x8, blocking collectives: none -> 80.1 us
    all_gather x0 -> x4, blocking collectives: none -> 60.2 us  [over_axes(): x = jnp.sum(lax.all_gather(x, axis), axis=0)]
    all_to_all x2, waiting for transfers between devices: 23.7 us -> 12.1 us  [sum_at_owner(): parts = lax.all_to_all(in_blocks(x, dim, count), axis, 0, 0, tiled=True)]
    all_to_all x1, waiting for transfers between devices: 10.7 us -> 0.01 us  [sent_to_all(): return lax.all_to_all(copies, axis, split_axis=0, concat_axis=0, tiled=True)]
    all_to_all x2, starting transfers between devices: 8.93 us -> 19.4 us  [sum_at_owner(): parts = lax.all_to_all(in_blocks(x, dim, count), axis, 0, 0, tiled=True)]
    unnamed x15 -> x47, local copies, waits for them, and re-layouts: 0.7 us -> 8.7 us
    all_to_all x2, blocking collectives: 45.6 us -> 42.2 us  [sent_to_all(): return lax.all_to_all(copies, axis, split_axis=0, concat_axis=0, tiled=True)]
  transfers between devices with their start and end apart: 3 -> 3, of which waited for: 3 -> 1; matrix products, arithmetic and copies ran while one was open for 0% -> 6% of each run, Pallas kernels for 0% -> 0%
where the time goes in v1:
time: 281 us; the launch traced here: 280 us
  blocking collectives  183 us (65%)
  starting transfers between devices  34.2 us (12%)
  other arithmetic  23.1 us (8%)
  local copies, waits for them, and re-layouts  12.8 us (5%)
  waiting for transfers between devices  12.1 us (4%)
  matrix products  9.43 us (3%)
  between operations  5.55 us (2%)
    unnamed x8, blocking collectives  80.1 us
    all_gather x4, blocking collectives, over_axes(): x = jnp.sum(lax.all_gather(x, axis), axis=0)  60.2 us
    all_to_all x2, blocking collectives, sent_to_all(): return lax.all_to_all(copies, axis, split_axis=0, concat_axis=0, tiled=True)  42.2 us
    all_to_all x2, starting transfers between devices, sum_at_owner(): parts = lax.all_to_all(in_blocks(x, dim, count), axis, 0, 0, tiled=True)  19.4 us
    all_to_all x1, starting transfers between devices, sent_to_all(): return lax.all_to_all(copies, axis, split_axis=0, concat_axis=0, tiled=True)  14.8 us
    all_to_all x2, waiting for transfers between devices, sum_at_owner(): parts = lax.all_to_all(in_blocks(x, dim, count), axis, 0, 0, tiled=True)  12.1 us
    another operation x6, other arithmetic, solve_small(): jnp.linalg.cholesky(gram_matrix + ridge * jnp.eye(order, dtype=gram_matri...  10.5 us
    another operation x4, other arithmetic, solve_small(): lax.linalg.triangular_solve(factor, halfway, left_side=True, lower=True,...  8.96 us
  transfers between devices with their start and end apart: 3, of which 1 were waited for; matrix products, arithmetic and copies ran while one was open for 6% of the time, Pallas kernels for 0%

profile of v1, /device:TPU:1, one launch (start us, length us, event | category | flops | bytes accessed | tf_op | source)
XLA Modules:
  0.0 279.8 jit_solution(9695604765951043781)
XLA Ops:
  0.7 0.8 convert_bitcast_fusion.2
  1.5 0.7 broadcast_in_dim.50
  2.3 14.8 %all-to-all-start = ((bf16[64,4,3,128]{3,1,2,0:T(4,128)(2,1)}), bf16[64,4,3,128]{3,1,2,0:T(4,128)(2,1)S(1)}, u32[]{:S(2)}, u32[]{:S(2)}) async-start(bf16[64,4,3,128]{3,1,2,0:T(4,128)(2,1)} %broadcast_in_dim.50), calls=%async_computation | async-start | bytes 393216 | tf_op jit(solution)/shard_map/all_to_all | solution.py:21
  17.1 1.5 convolution_bitcast_fusion
  18.6 20.6 %all-gather.16 = f32[8,50,50]{2,1,0:T(8,128)S(1)} all-gather(f32[1,50,50]{2,1,0:T(8,128)S(1)} %convolution_bitcast_fusion), channel_id=2, replica_groups=mesh['fluid_0'=8,'fluid_1'=4,'fluid_2'=2,'solid'=8] {'fluid_0'}, dimensions={0}, use_global_device_ids=true | all-gather | bytes 90000 | tf_op jit(solution)/shard_map/all_gather | solution.py:15
  39.2 9.3 %all-gather.17 = f32[4,50,50]{2,1,0:T(8,128)S(1)} all-gather(f32[1,50,50]{2,1,0:T(8,128)S(1)} %bitcast.174), channel_id=3, replica_groups=mesh['fluid_0'=8,'fluid_1'=4,'fluid_2'=2,'solid'=8] {'fluid_1'}, dimensions={0}, use_global_device_ids=true | all-gather | bytes 50000 | tf_op jit(solution)/shard_map/all_gather | solution.py:15
  48.5 10.3 %all-gather.18 = f32[2,50,50]{2,1,0:T(8,128)S(1)} all-gather(f32[1,50,50]{2,1,0:T(8,128)S(1)} %bitcast.175), channel_id=4, replica_groups=mesh['fluid_0'=8,'fluid_1'=4,'fluid_2'=2,'solid'=8] {'fluid_2'}, dimensions={0}, use_global_device_ids=true | all-gather | bytes 30000 | tf_op jit(solution)/shard_map/all_gather | solution.py:15
  58.9 20.0 %all-gather.19 = f32[8,50,50]{2,1,0:T(8,128)S(1)} all-gather(f32[1,50,50]{2,1,0:T(8,128)S(1)} %bitcast.176), channel_id=5, replica_groups=mesh['fluid_0'=8,'fluid_1'=4,'fluid_2'=2,'solid'=8] {'solid'}, dimensions={0}, use_global_device_ids=true | all-gather | bytes 90000 | tf_op jit(solution)/shard_map/all_gather | solution.py:15
  79.0 0.6 select_reduce_fusion.3
  80.4 4.6 %cholesky.44 = f32[50,50]{1,0:T(8,128)S(1)} custom-call(f32[50,50]{1,0:T(8,128)S(1)} %fusion.54), custom_call_target="Cholesky" | custom-call | tf_op jit(solution)/shard_map/jit(cholesky)/cholesky | solution.py:49
  85.7 0.2 convolution_convert_fusion.4
  86.0 1.7 fusion.9
  87.7 0.5 convolution_convert_fusion.1
  88.2 0.7 copy.85
  88.9 14.8 %all-to-all-start.1 = ((bf16[64,4,3,128]{3,1,2,0:T(4,128)(2,1)}), bf16[64,4,3,128]{3,1,2,0:T(4,128)(2,1)S(1)}, u32[]{:S(2)}, u32[]{:S(2)}) async-start(bf16[64,4,3,128]{3,1,2,0:T(4,128)(2,1)} %copy.85), calls=%async_computation.1 | async-start | bytes 393216 | tf_op jit(solution)/shard_map/all_to_all | solution.py:42
  103.8 0.6 compare_reduce_fusion.1
  104.4 0.7 fusion.47
  105.1 3.8 %custom-call.11 = f32[1,50,50]{1,2,0:T(8,128)S(1)} custom-call(f32[1,50,50]{2,1,0:T(8,128)S(1)} %fusion.47), custom_call_target="InvertDiagBlocksLowerTriangular" | custom-call | tf_op jit(solution)/shard_map/triangular_solve/custom-call.2 | solution.py:51
  108.9 1.3 dynamic-slice
  110.2 1.3 dynamic-slice.1
  112.7 1.3 dynamic-slice.2
  114.7 1.3 dynamic-slice.3
  116.8 0.4 convolution_bitcast_fusion.3
  117.2 0.2 dynamic-update-slice.2
  117.4 13.5 %all-reduce = f32[400]{0:T(512)S(1)} all-reduce(f32[400]{0:T(512)S(1)} %dynamic-update-slice.2), channel_id=6, replica_groups=mesh['fluid_0'=8,'fluid_1'=4,'fluid_2'=2,'solid'=8] {'fluid_0'}, use_global_device_ids=true, to_apply=%add | all-reduce | flops 400 | bytes 3200
  131.0 0.2 dynamic-update-slice.3
  131.2 8.4 %all-reduce.1 = f32[200]{0:T(256)S(1)} all-reduce(f32[200]{0:T(256)S(1)} %dynamic-update-slice.3), channel_id=7, replica_groups=mesh['fluid_0'=8,'fluid_1'=4,'fluid_2'=2,'solid'=8] {'fluid_1'}, use_global_device_ids=true, to_apply=%add.1 | all-reduce | flops 200 | bytes 1600
  139.7 0.2 dynamic-update-slice.4
  140.0 8.3 %all-reduce.2 = f32[100]{0:T(128)S(1)} all-reduce(f32[100]{0:T(128)S(1)} %dynamic-update-slice.4), channel_id=8, replica_groups=mesh['fluid_0'=8,'fluid_1'=4,'fluid_2'=2,'solid'=8] {'fluid_2'}, use_global_device_ids=true, to_apply=%add.2 | all-reduce | flops 100 | bytes 800
  148.3 0.2 dynamic-update-slice.5
  148.6 12.2 %all-reduce.3 = f32[400]{0:T(512)S(1)} all-reduce(f32[400]{0:T(512)S(1)} %dynamic-update-slice.5), channel_id=9, replica_groups=mesh['fluid_0'=8,'fluid_1'=4,'fluid_2'=2,'solid'=8] {'solid'}, use_global_device_ids=true, to_apply=%add.3 | all-reduce | flops 400 | bytes 3200
  161.1 0.3 fusion.16
  161.5 21.2 %all_to_all.25 = bf16[64,4,3,128]{3,1,2,0:T(4,128)(2,1)S(1)} all-to-all(bf16[64,4,3,128]{3,1,2,0:T(4,128)(2,1)S(1)} %broadcast_in_dim.54), channel_id=1, replica_groups=mesh['fluid_0'=8,'fluid_1'=4,'fluid_2'=2,'solid'=8] {'fluid_0','fluid_1'..., dimensions={0} | all-to-all | bytes 393216 | tf_op jit(solution)/shard_map/all_to_all | solution.py:21
  182.8 0.2 convolution_convert_fusion.3
  183.0 1.7 fusion.8
  184.7 0.5 convolution_convert_fusion
  185.2 0.7 copy.96
  185.9 4.6 %all-to-all-start.3 = ((bf16[64,4,3,128]{3,1,2,0:T(4,128)(2,1)}), bf16[64,4,3,128]{3,1,2,0:T(4,128)(2,1)S(1)}, u32[]{:S(2)}, u32[]{:S(2)}) async-start(bf16[64,4,3,128]{3,1,2,0:T(4,128)(2,1)} %copy.96), calls=%async_computation.3 | async-start | bytes 393216 | tf_op jit(solution)/shard_map/all_to_all | solution.py:42
  190.7 12.1 %all-to-all-done.3 = bf16[64,4,3,128]{3,1,2,0:T(4,128)(2,1)S(1)} async-done(((bf16[64,4,3,128]{3,1,2,0:T(4,128)(2,1)}), bf16[64,4,3,128]{3,1,2,0:T(4,128)(2,1)S(1)}, u32[]{:S(2)}, u32[]{:S(2)}) %all-to-all-start.3) | async-done | bytes 196640 | tf_op jit(solution)/shard_map/all_to_all | solution.py:42
  203.0 0.4 convolution_bitcast_fusion.1
  203.4 0.4 convolution_bitcast_fusion.2
  203.8 0.2 dynamic-update-slice.10
  204.0 0.2 dynamic-update-slice.6
  204.2 11.3 %all-reduce.13 = (f32[400]{0:T(512)S(1)}, f32[400]{0:T(512)S(1)}) all-reduce(f32[400]{0:T(512)S(1)} %dynamic-update-slice.6, f32[400]{0:T(512)S(1)} %dynamic-update-slice.10), channel_id=10, replica_groups=mesh['fluid_0'=8,'fluid_1'=4,'fluid_2'=2,'solid'=8] {'fluid_0'}, use_global_device_ids=true, to_apply=%add.4 | all-reduce | flops 800 | bytes 6400
  215.7 0.2 dynamic-update-slice.11
  215.9 0.2 dynamic-update-slice.7
  216.2 6.8 %all-reduce.14 = (f32[200]{0:T(256)S(1)}, f32[200]{0:T(256)S(1)}) all-reduce(f32[200]{0:T(256)S(1)} %dynamic-update-slice.7, f32[200]{0:T(256)S(1)} %dynamic-update-slice.11), channel_id=11, replica_groups=mesh['fluid_0'=8,'fluid_1'=4,'fluid_2'=2,'solid'=8] {'fluid_1'}, use_global_device_ids=true, to_apply=%add.5 | all-reduce | flops 400 | bytes 3200
  223.2 0.2 dynamic-update-slice.12
  223.4 0.2 dynamic-update-slice.8
  223.7 8.5 %all-reduce.15 = (f32[100]{0:T(128)S(1)}, f32[100]{0:T(128)S(1)}) all-reduce(f32[100]{0:T(128)S(1)} %dynamic-update-slice.8, f32[100]{0:T(128)S(1)} %dynamic-update-slice.12), channel_id=12, replica_groups=mesh['fluid_0'=8,'fluid_1'=4,'fluid_2'=2,'solid'=8] {'fluid_2'}, use_global_device_ids=true, to_apply=%add.6 | all-reduce | flops 200 | bytes 1600
  232.4 0.2 dynamic-update-slice.13
  232.7 0.2 dynamic-update-slice.9
  232.9 11.2 %all-reduce.12 = (f32[400]{0:T(512)S(1)}, f32[400]{0:T(512)S(1)}) all-reduce(f32[400]{0:T(512)S(1)} %dynamic-update-slice.9, f32[400]{0:T(512)S(1)} %dynamic-update-slice.13), channel_id=13, replica_groups=mesh['fluid_0'=8,'fluid_1'=4,'fluid_2'=2,'solid'=8] {'solid'}, use_global_device_ids=true, to_apply=%add.7 | all-reduce | flops 800 | bytes 6400
  244.3 0.7 select_reduce_fusion.2
  245.9 4.6 %cholesky.55 = f32[50,50]{1,0:T(8,128)S(1)} custom-call(f32[50,50]{1,0:T(8,128)S(1)} %fusion.51), custom_call_target="Cholesky" | custom-call | tf_op jit(solution)/shard_map/jit(cholesky)/cholesky | solution.py:49
  250.5 0.6 compare_reduce_fusion
  251.2 0.7 fusion.48
  251.8 3.8 %custom-call.13 = f32[1,50,50]{1,2,0:T(8,128)S(1)} custom-call(f32[1,50,50]{2,1,0:T(8,128)S(1)} %fusion.48), custom_call_target="InvertDiagBlocksLowerTriangular" | custom-call | tf_op jit(solution)/shard_map/triangular_solve/custom-call.2 | solution.py:51
  256.2 0.3 fusion.14
  256.5 0.6 convert_bitcast_fusion
  257.1 21.1 %all_to_all.26 = bf16[64,4,3,128]{3,1,2,0:T(4,128)(2,1)S(1)} all-to-all(bf16[64,4,3,128]{3,1,2,0:T(4,128)(2,1)S(1)} %broadcast_in_dim.61), channel_id=1, replica_groups=mesh['fluid_0'=8,'fluid_1'=4,'fluid_2'=2,'solid'=8] {'fluid_0','fluid_1'..., dimensions={0} | all-to-all | bytes 393216 | tf_op jit(solution)/shard_map/all_to_all | solution.py:21
  278.3 0.2 convolution_convert_fusion.2
  278.5 0.7 convolution_multiply_fusion
  279.1 0.7 copy.102
  (93 shorter events, 3.5 us)
Async XLA Ops:
  0.6 85.3 %copy-start = (bf16[64,128,128]{2,1,0:T(8,128)(2,1)S(1)}, bf16[64,128,128]{2,1,0:T(8,128)(2,1)}, u32[]{:S(2)}) copy-start(bf16[64,128,128]{2,1,0:T(8,128)(2,1)} %param.17) | copy-start | bytes 6291460
  0.6 85.0 %copy-start.8 = (s32[64,1]{0,1:T(1,128)S(1)}, s32[64,1]{0,1:T(1,128)}, u32[]{:S(2)}) copy-start(s32[64,1]{0,1:T(1,128)} %param.19) | copy-start | bytes 772
  0.7 85.0 %copy-start.7 = (s32[64]{0:T(128)S(1)}, s32[64]{0:T(128)}, u32[]{:S(2)}) copy-start(s32[64]{0:T(128)} %param.20) | copy-start | bytes 772
  0.7 85.3 %copy-start.3 = (f32[64,3,128]{2,0,1:T(8,128)S(1)}, f32[64,3,128]{2,0,1:T(8,128)}, u32[]{:S(2)}) copy-start(f32[64,3,128]{2,0,1:T(8,128)} %param.15) | copy-start | bytes 294916
  0.7 85.3 %copy-start.4 = (f32[64,3,128]{2,0,1:T(8,128)S(1)}, f32[64,3,128]{2,0,1:T(8,128)}, u32[]{:S(2)}) copy-start(f32[64,3,128]{2,0,1:T(8,128)} %param.16) | copy-start | bytes 294916
  2.3 83.4 %all-to-all-start = ((bf16[64,4,3,128]{3,1,2,0:T(4,128)(2,1)}), bf16[64,4,3,128]{3,1,2,0:T(4,128)(2,1)S(1)}, u32[]{:S(2)}, u32[]{:S(2)}) async-start(bf16[64,4,3,128]{3,1,2,0:T(4,128)(2,1)} %broadcast_in_dim.50), calls=%async_computation | async-start | bytes 393216 | tf_op jit(solution)/shard_map/all_to_all | solution.py:21
  86.0 30.8 %copy-start.5 = (f32[1,4,3,128]{3,1,2,0:T(4,128)S(1)}, f32[1,4,3,128]{3,1,2,0:T(4,128)}, u32[]{:S(2)}) copy-start(f32[1,4,3,128]{3,1,2,0:T(4,128)} %param.21) | copy-start | bytes 18436
  86.0 30.8 %copy-start.6 = (f32[1,4,3,128]{3,1,2,0:T(4,128)S(1)}, f32[1,4,3,128]{3,1,2,0:T(4,128)}, u32[]{:S(2)}) copy-start(f32[1,4,3,128]{3,1,2,0:T(4,128)} %param.22) | copy-start | bytes 18436
  86.0 30.8 %copy-start.1 = (f32[50,1,4,3,128]{4,2,3,1,0:T(4,128)S(1)}, f32[50,1,4,3,128]{4,2,3,1,0:T(4,128)}, u32[]{:S(2)}) copy-start(f32[50,1,4,3,128]{4,2,3,1,0:T(4,128)} %param.23) | copy-start | bytes 921604
  87.7 73.4 %copy-start.2 = (f32[50,1,4,3,128]{4,2,3,1,0:T(4,128)S(1)}, f32[50,1,4,3,128]{4,2,3,1,0:T(4,128)}, u32[]{:S(2)}) copy-start(f32[50,1,4,3,128]{4,2,3,1,0:T(4,128)} %param.24) | copy-start | bytes 921604
  88.9 27.7 %all-to-all-start.1 = ((bf16[64,4,3,128]{3,1,2,0:T(4,128)(2,1)}), bf16[64,4,3,128]{3,1,2,0:T(4,128)(2,1)S(1)}, u32[]{:S(2)}, u32[]{:S(2)}) async-start(bf16[64,4,3,128]{3,1,2,0:T(4,128)(2,1)} %copy.85), calls=%async_computation.1 | async-start | bytes 393216 | tf_op jit(solution)/shard_map/all_to_all | solution.py:42
  185.9 16.9 %all-to-all-start.3 = ((bf16[64,4,3,128]{3,1,2,0:T(4,128)(2,1)}), bf16[64,4,3,128]{3,1,2,0:T(4,128)(2,1)S(1)}, u32[]{:S(2)}, u32[]{:S(2)}) async-start(bf16[64,4,3,128]{3,1,2,0:T(4,128)(2,1)} %copy.96), calls=%async_computation.3 | async-start | bytes 393216 | tf_op jit(solution)/shard_map/all_to_all | solution.py:42
